TPU v7x, 32 devices: a whole 2x2x4 slice. The times are simulated.
32 devices in a mesh: dp: 4 (over z), fsdp: 8 (over y, x, core).
Axes of the slice: x: 2, y: 2, z: 4, core: 2. Of those that a mesh axis runs over, the one named last changes fastest.
Arguments:
- hidden: bfloat16 [8192, 4096], P(('dp', 'fsdp')), may hold values from -6 to 6
- queries: bfloat16 [8192, 2048], P(('dp', 'fsdp')), may hold values from -6 to 6
- keys: bfloat16 [8192, 512], P(('dp', 'fsdp')), may hold values from -6 to 6
- target: bfloat16 [8192, 2048], P(('dp', 'fsdp')), may hold values from -6 to 6
- lengths: int32 [32], P(('dp', 'fsdp')), may hold values from 64 to 256
- value_weight_frozen: bfloat16 [4096, 512], P('fsdp'), may hold values from -0.09375 to 0.09375
- adapter_down_map: float32 [4096, 64], P('fsdp'), may hold values from -0.09375 to 0.09375
- adapter_up_map: float32 [64, 512], replicated, may hold values from -0.75 to 0.75
- average_down_map: float32 [4096, 64], P('fsdp'), may hold values from -0.09375 to 0.09375
- average_up_map: float32 [64, 512], replicated, may hold values from -0.75 to 0.75
Outputs:
- down_map_gradient: float32 [4096, 64], P('fsdp')
- up_map_gradient: float32 [64, 512], replicated
- average_down_next: float32 [4096, 64], P('fsdp')
- average_up_next: float32 [64, 512], replicated
- loss: float32 [], replicated
Inputs may be any that keep to these rules, and one draw needn't show every extreme that they name: `lengths`: slots at or past a sequence's length are padding.
All inputs are finite; a program needn't handle non-finite values.
Results may differ from a plain program's by a relative error of at most 0.0049.
Values may be sent and summed in bfloat16 or wider, within the bound.
A program may use at most 64 MiB of HBM per device.

v0:
```python
import math
import jax
import jax.numpy as jnp
from jax import lax
from jax.sharding import PartitionSpec as P

HEADS = 16
KEY_VALUE_HEADS = 4
HEAD_DIM = 128
adapter_scale = 2.0
average_decay = 0.9
learning_rate = 1.0
masked_score = -1e30


def per_device(
    hidden,
    queries,
    keys,
    target,
    lengths,
    value_weight_frozen,
    adapter_down_map,
    adapter_up_map,
    average_down_map,
    average_up_map,
):
    tok_rows = hidden.shape[0]
    group_size = HEADS // KEY_VALUE_HEADS
    seq_length = lengths[0]
    down_factor_slice = adapter_down_map.astype(jnp.bfloat16)
    up_factor_slice = adapter_up_map.astype(jnp.bfloat16)
    columns = hidden
    frozen_value_output = jnp.dot(
        columns,
        lax.all_gather(value_weight_frozen, "fsdp", axis=0, tiled=True),
        preferred_element_type=jnp.float32,
    )
    adapter_hidden = jnp.dot(
        columns,
        lax.all_gather(down_factor_slice, "fsdp", axis=0, tiled=True),
        preferred_element_type=jnp.float32,
    )
    adapter_hidden = adapter_hidden.astype(jnp.bfloat16)
    value_outputs = (
        frozen_value_output
        + adapter_scale
        * jnp.dot(adapter_hidden, up_factor_slice, preferred_element_type=jnp.float32)
    ).astype(jnp.bfloat16)
    position = jnp.arange(tok_rows, dtype=jnp.int32)
    allowed = (position[None, :] <= position[:, None]) & (position[None, :] < seq_length)
    q_heads = queries.reshape(tok_rows, KEY_VALUE_HEADS, group_size, HEAD_DIM)
    k_heads = keys.reshape(tok_rows, KEY_VALUE_HEADS, HEAD_DIM)
    v_heads = value_outputs.reshape(tok_rows, KEY_VALUE_HEADS, HEAD_DIM)
    scores = jnp.einsum(
        "tkgd,skd->kgts", q_heads, k_heads, preferred_element_type=jnp.float32
    ) / math.sqrt(HEAD_DIM)
    scores = jnp.where(allowed, scores, masked_score)
    row_max = jnp.max(scores, axis=-1, keepdims=True)
    weights = jnp.exp(scores - row_max)
    attn_probs = (weights / jnp.sum(weights, axis=-1, keepdims=True)).astype(jnp.bfloat16)
    output = jnp.einsum(
        "kgts,skd->tkgd", attn_probs, v_heads, preferred_element_type=jnp.float32
    ).reshape(tok_rows, HEADS * HEAD_DIM)
    live_rows = (position < seq_length)[:, None]
    differ = jnp.where(live_rows, output - target.astype(jnp.float32), 0.0)
    loss_local = jnp.sum(differ * differ)
    cotangent = differ.astype(jnp.bfloat16).reshape(tok_rows, KEY_VALUE_HEADS, group_size, HEAD_DIM)
    value_grad = jnp.einsum(
        "kgts,tkgd->skd", attn_probs, cotangent, preferred_element_type=jnp.float32
    )
    value_grad = value_grad.reshape(tok_rows, KEY_VALUE_HEADS * HEAD_DIM).astype(jnp.bfloat16)
    latent_grad = lax.dot_general(
        value_grad, up_factor_slice, (((1,), (1,)), ((), ())), preferred_element_type=jnp.float32
    ).astype(jnp.bfloat16)
    up_term = lax.dot_general(
        adapter_hidden, value_grad, (((0,), (0,)), ((), ())), preferred_element_type=jnp.float32
    )
    count_local = seq_length.astype(jnp.float32)
    columns = hidden
    down_map_gradient = lax.psum(
        adapter_scale
        * lax.dot_general(
            columns, latent_grad, (((0,), (0,)), ((), ())), preferred_element_type=jnp.float32
        ),
        "dp",
    )
    down_map_gradient = lax.psum_scatter(down_map_gradient, "fsdp", scatter_dimension=0, tiled=True)
    up_map_gradient, loss_sum, token_grand_count = lax.psum(
        (adapter_scale * up_term, loss_local, count_local), ("dp", "fsdp")
    )
    up_map_gradient = up_map_gradient / token_grand_count
    down_map_gradient = down_map_gradient / token_grand_count
    loss = loss_sum / (2.0 * token_grand_count)
    average_down_next = average_decay * average_down_map + (1.0 - average_decay) * (
        adapter_down_map - learning_rate * down_map_gradient
    )
    average_up_next = average_decay * average_up_map + (1.0 - average_decay) * (
        adapter_up_map - learning_rate * up_map_gradient
    )
    return (down_map_gradient, up_map_gradient, average_down_next, average_up_next, loss)


def solution(mesh):
    placed = (
        P(("dp", "fsdp"), None),
        P(("dp", "fsdp"), None),
        P(("dp", "fsdp"), None),
        P(("dp", "fsdp"), None),
        P(("dp", "fsdp")),
        P("fsdp", None),
        P("fsdp", None),
        P(),
        P("fsdp", None),
        P(),
    )
    return jax.shard_map(
        per_device,
        mesh=mesh,
        in_specs=placed,
        out_specs=(P("fsdp", None), P(), P("fsdp", None), P(), P()),
        check_vma=False,
    )
```

profile of v0, /device:TPU:0, one launch (start us, length us, event | category | flops | bytes accessed | tf_op | source)
XLA Modules:
  0.0 281.5 jit_solution(8382225691264275477)
XLA Ops:
  7.2 0.0 copy-start
  7.2 0.0 copy-start.3
  7.2 0.0 all-gather.2.cloned.1.call-start
  7.2 0.7 all-gather.2.cloned.1.call-update
  7.9 0.0 reduce-scatter.2.cloned.1.call-start
  8.6 1.8 reshape.40
  10.4 1.0 reshape.39
  11.4 0.0 copy-done.3
  11.5 11.3 %all_gather.7 = bf16[4096,64]{0,1:T(8,128)(2,1)S(1)} all-gather(bf16[512,64]{0,1:T(8,128)(2,1)S(1)} %convert_element_type.36), channel_id=1, replica_groups=mesh['dp'=4,'fsdp'=8] {'fsdp'}, dimensions={0}, use_global_device_ids=true | all-gather | bytes 589824 | tf_op jit(solution)/shard_map/all_gather | solution.py:41
  22.8 0.1 fusion.13
  22.9 0.0 copy-done
  22.9 1.4 convolution_convert_fusion.1
  24.3 0.7 fusion.10
  25.0 1.2 fusion.19
  26.3 1.8 divide_convert_fusion
  28.0 21.2 %all-gather.2.cloned.1.call-done = bf16[4096,512]{1,0:T(8,128)(2,1)} async-done(((bf16[512,512]{1,0:T(8,128)(2,1)}), bf16[4096,512]{1,0:T(8,128)(2,1)}) %all-gather.2.cloned.1.call-update) | async-done | bytes 4194320 | tf_op jit(solution)/shard_map/all_gather | solution.py:36
  49.2 3.4 %fusion.20 = f32[256,512]{1,0:T(8,128)S(1)} fusion(bf16[256,4096]{1,0:T(8,128)(2,1)S(1)} %copy-done, bf16[4096,512]{1,0:T(8,128)(2,1)} %all-gather.2.cloned.1.call-done), kind=kOutput, calls=%fused_computation.36 | convolution fusion | flops 1073741824 | bytes 6815744 | tf_op jit(solution)/shard_map/dot_general | solution.py:34
  52.7 0.0 copy-done.1
  52.7 0.0 copy-done.5
  52.7 0.3 fusion.8
  52.9 0.1 copy.27
  53.1 3.3 %fusion.21 = f32[4,128,4,256]{3,1,2,0:T(8,128)} fusion(bf16[256,4,128,1]{0,2,3,1:T(8,128)(2,1)S(1)} %bitcast.51, bf16[4,4,256,256]{2,3,1,0:T(8,128)(2,1)} %divide_convert_fusion), kind=kOutput, calls=%fused_computation.37 | convolution fusion | flops 268435456 | bytes 4456448 | tf_op jit(solution)/shard_map/kgts,skd->tkgd/dot_general | solution.py:62
  56.4 3.0 %copy.19 = f32[256,2048]{1,0:T(8,128)} copy(f32[256,2048]{0,1:T(8,128)} %bitcast.47) | data formatting | bytes 4194304 | tf_op jit(solution)/shard_map/reshape | solution.py:64
  59.5 0.0 copy-done.2
  59.5 3.6 %multiply_reduce_fusion = (f32[]{:T(128)}, bf16[256,2048]{1,0:T(8,128)(2,1)}) fusion(f32[256,2048]{1,0:T(8,128)} %copy.19, bf16[256,2048]{1,0:T(8,128)(2,1)S(1)} %copy-done.2, pred[256]{0:T(512)(128)(4,1)S(1)} %iota_compare_fusion.1), kind=kLoop, calls=%fused_computation.7 | loop fusion | flops 3145727 | bytes 4194564 | tf_op jit(solution)/shard_map/reduce_sum | solution.py:67
  63.1 1.5 copy.30
  64.6 2.4 fusion.9
  67.0 0.0 copy-start.6
  67.0 0.0 copy-start.7
  67.0 0.0 copy-start.4
  67.0 0.0 copy-start.8
  67.0 1.8 fusion.1
  68.9 0.0 reduce-scatter.2.cloned.1.call-update
  68.9 0.0 all-reduce.4.cloned.1.call-start
  68.9 0.0 copy-done.6
  69.0 0.9 convolution_multiply_fusion.2
  69.8 0.0 all-reduce.4.cloned.1.call-update
  69.8 0.0 all-reduce.6.cloned.1.call-start
  69.9 39.5 %all-reduce = (f32[]{:T(128)}, f32[]{:T(128)}) all-reduce(f32[]{:T(128)S(6)} %convert_element_type.47, f32[]{:T(128)} %get-tuple-element.11), channel_id=1, replica_groups=mesh['dp'=4,'fsdp'=8] {'dp','fsdp'}, use_global_device_ids=true, to_apply=%region_4.5 | all-reduce | flops 2 | bytes 16 | tf_op jit(solution)/shard_map/psum | solution.py:89
  110.7 0.0 reduce-scatter.2.cloned.1.call-done
  110.7 0.0 all-reduce.6.cloned.1.call-update
  110.7 125.1 %all-reduce.4.cloned.1.call-done = f32[64,512]{1,0:T(8,128)} async-done(((f32[64,512]{1,0:T(8,128)}), f32[64,512]{1,0:T(8,128)}) %all-reduce.4.cloned.1.call-update) | async-done | bytes 131088 | tf_op jit(solution)/shard_map/psum | solution.py:89
  235.8 0.0 copy-done.7
  235.8 2.2 multiply_add_fusion
  238.0 33.7 %all-reduce.6.cloned.1.call-done = f32[512,64]{0,1:T(8,128)} async-done(((f32[512,64]{0,1:T(8,128)}), f32[512,64]{0,1:T(8,128)}) %all-reduce.6.cloned.1.call-update) | async-done | bytes 131088 | tf_op jit(solution)/shard_map/psum | solution.py:81
  271.7 0.0 copy-done.4
  271.7 0.0 copy-done.8
  271.7 2.2 multiply_add_fusion.1
  (5 shorter events, 0.0 us)
Async XLA Ops:
  7.2 15.8 %copy-start = (bf16[256,4096]{1,0:T(8,128)(2,1)S(1)}, bf16[256,4096]{1,0:T(8,128)(2,1)}, u32[]{:S(2)}) copy-start(bf16[256,4096]{1,0:T(8,128)(2,1)} %param.10) | copy-start | bytes 6291460
  7.2 4.3 %copy-start.3 = (f32[512,64]{0,1:T(8,128)S(1)}, f32[512,64]{0,1:T(8,128)}, u32[]{:S(2)}) copy-start(f32[512,64]{0,1:T(8,128)} %param.16) | copy-start | bytes 393220
  7.2 42.0 %all-gather.2.cloned.1.call-start = ((), (), s32[]{:S(2)}) async-start(), calls=%async_computation.1 | async-start | bytes 4718592 | tf_op jit(solution)/shard_map/all_gather | solution.py:36
  7.9 102.8 %reduce-scatter.2.cloned.1.call-start = ((), (), s32[]{:S(2)}) async-start(), calls=%async_computation.3 | async-start | bytes 1179648 | tf_op jit(solution)/shard_map/reduce_scatter | solution.py:88
  28.0 24.6 %copy-start.1 = (f32[64,512]{1,0:T(8,128)S(1)}, f32[64,512]{1,0:T(8,128)}, u32[]{:S(2)}) copy-start(f32[64,512]{1,0:T(8,128)} %param.17) | copy-start | bytes 393220
  28.0 24.6 %copy-start.5 = (bf16[256,64]{0,1:T(8,128)(2,1)S(1)}, bf16[256,64]{0,1:T(8,128)(2,1)}, u32[]{:S(2)}) copy-start(bf16[256,64]{0,1:T(8,128)(2,1)} %convolution_convert_fusion.1) | copy-start | bytes 98308
  56.4 3.0 %copy-start.2 = (bf16[256,2048]{1,0:T(8,128)(2,1)S(1)}, bf16[256,2048]{1,0:T(8,128)(2,1)}, u32[]{:S(2)}) copy-start(bf16[256,2048]{1,0:T(8,128)(2,1)} %param.13) | copy-start | bytes 3145732
  67.0 2.0 copy-start.6
  67.0 168.8 %copy-start.7 = (f32[64,512]{1,0:T(8,128)S(1)}, f32[64,512]{1,0:T(8,128)}, u32[]{:S(2)}) copy-start(f32[64,512]{1,0:T(8,128)} %param.19) | copy-start | bytes 393220
  67.0 204.7 %copy-start.4 = (f32[512,64]{0,1:T(8,128)S(1)}, f32[512,64]{0,1:T(8,128)}, u32[]{:S(2)}) copy-start(f32[512,64]{0,1:T(8,128)} %param.16) | copy-start | bytes 393220
  67.0 204.7 %copy-start.8 = (f32[512,64]{0,1:T(8,128)S(1)}, f32[512,64]{0,1:T(8,128)}, u32[]{:S(2)}) copy-start(f32[512,64]{0,1:T(8,128)} %param.18) | copy-start | bytes 393220
  68.9 166.9 %all-reduce.4.cloned.1.call-start = ((), (), s32[]{:S(2)}) async-start(), calls=%async_computation.2 | async-start | bytes 262144 | tf_op jit(solution)/shard_map/psum | solution.py:89
  69.8 201.8 %all-reduce.6.cloned.1.call-start = ((), (), s32[]{:S(2)}) async-start(), calls=%async_computation.4 | async-start | bytes 262144 | tf_op jit(solution)/shard_map/psum | solution.py:81
Sparse Core Ops, SparseCore 0:
  9.9 39.2 all-gather.1
  69.0 35.9 reduce-scatter.1
  111.1 124.5 all-reduce.3
  237.9 33.6 all-reduce.5
where the time goes:
time: 282 us
  waiting for transfers between devices  181 us (64%)
  blocking collectives  50.9 us (18%)
  between operations  16.9 us (6%)
  matrix products  14.2 us (5%)
  other arithmetic  11.1 us (4%)
  local copies, waits for them, and re-layouts  7.48 us (3%)
    psum x1, waiting for transfers between devices, per_device(): lax.psum((adapter_scale * up_term, loss_local, count_local), ('dp', 'fsdp'))  125 us
    psum x1, blocking collectives, per_device(): lax.psum((adapter_scale * up_term, loss_local, count_local), ('dp', 'fsdp'))  39.5 us
    psum x1, waiting for transfers between devices, per_device(): lax.psum(adapter_scale * lax.dot_general(columns, latent_grad, (((0,), (0...  33.7 us
    all_gather x1, waiting for transfers between devices, per_device(): lax.all_gather(value_weight_frozen, 'fsdp', axis=0, tiled=True)  21.2 us
    all_gather x1, blocking collectives, per_device(): lax.all_gather(down_factor_slice, 'fsdp', axis=0, tiled=True)  11.3 us
  transfers between devices with their start and end apart: 4, of which 3 were waited for; matrix products, arithmetic and copies ran while one was open for 4% of the time, Pallas kernels for 0%

commit v1 on v0

--- a/solution.py
+++ b/solution.py
@@ -11,6 +11,12 @@
 average_decay = 0.9
 learning_rate = 1.0
 masked_score = -1e30
+
+
+def _carry_members_all(sheet):
+    q_next = lax.all_gather(sheet, "dp")
+    right_arr = jnp.sum(q_next, 0)
+    return right_arr
 
 
 def per_device(
@@ -78,12 +84,11 @@
     )
     count_local = seq_length.astype(jnp.float32)
     columns = hidden
-    down_map_gradient = lax.psum(
+    down_map_gradient = _carry_members_all(
         adapter_scale
         * lax.dot_general(
             columns, latent_grad, (((0,), (0,)), ((), ())), preferred_element_type=jnp.float32
-        ),
-        "dp",
+        )
     )
     down_map_gradient = lax.psum_scatter(down_map_gradient, "fsdp", scatter_dimension=0, tiled=True)
     up_map_gradient, loss_sum, token_grand_count = lax.psum(

time: 282 us -> 327 us (1.16)
  waiting for transfers between devices: 181 us -> 215 us
  local copies, waits for them, and re-layouts: 7.48 us -> 13.5 us
  other arithmetic: 11.1 us -> 17 us
    all_gather x0 -> x1, waiting for transfers between devices: none -> 79.9 us  [_carry_members_all(): q_next = lax.all_gather(sheet, 'dp')]
    psum x1, waiting for transfers between devices: 125 us -> 77 us  [per_device(): lax.psum((adapter_scale * up_term, loss_local, count_local), ('dp', 'fsdp'))]
    reduce_scatter x1, waiting for transfers between devices: 0.02 us -> 35.8 us  [per_device(): lax.psum_scatter(down_map_gradient, 'fsdp', scatter_dimension=0, tiled=True)]
    psum x1 -> x0, waiting for transfers between devices: 33.7 us -> none  [per_device(): lax.psum(adapter_scale * lax.dot_general(columns, latent_grad, (((0,), (0...]
    all_gather x0 -> x1, local copies, waits for them, and re-layouts: none -> 6.05 us  [_carry_members_all(): q_next = lax.all_gather(sheet, 'dp')]
    reduce_sum x0 -> x1, other arithmetic: none -> 5.88 us  [_carry_members_all(): right_arr = jnp.sum(q_next, 0)]
  transfers between devices with their start and end apart: 4 -> 4, of which waited for: 3 -> 4; matrix products, arithmetic and copies ran while one was open for 4% -> 7% of each run, Pallas kernels for 0% -> 0%
where the time goes in v1:
time: 327 us
  waiting for transfers between devices  215 us (66%)
  blocking collectives  50.3 us (15%)
  other arithmetic  17 us (5%)
  between operations  16.9 us (5%)
  matrix products  14.2 us (4%)
  local copies, waits for them, and re-layouts  13.5 us (4%)
    all_gather x1, waiting for transfers between devices, _carry_members_all(): q_next = lax.all_gather(sheet, 'dp')  79.9 us
    psum x1, waiting for transfers between devices, per_device(): lax.psum((adapter_scale * up_term, loss_local, count_local), ('dp', 'fsdp'))  77 us
    psum x1, blocking collectives, per_device(): lax.psum((adapter_scale * up_term, loss_local, count_local), ('dp', 'fsdp'))  38.9 us
    reduce_scatter x1, waiting for transfers between devices, per_device(): lax.psum_scatter(down_map_gradient, 'fsdp', scatter_dimension=0, tiled=True)  35.8 us
    all_gather x1, waiting for transfers between devices, per_device(): lax.all_gather(value_weight_frozen, 'fsdp', axis=0, tiled=True)  21.2 us
    all_gather x1, blocking collectives, per_device(): lax.all_gather(down_factor_slice, 'fsdp', axis=0, tiled=True)  11.3 us
  transfers between devices with their start and end apart: 4, of which 4 were waited for; matrix products, arithmetic and copies ran while one was open for 7% of the time, Pallas kernels for 0%

profile of v1, /device:TPU:0, one launch (start us, length us, event | category | flops | bytes accessed | tf_op | source)
XLA Modules:
  0.0 326.8 jit_solution(15288402735363591970)
XLA Ops:
  7.2 0.0 copy-start
  7.2 0.0 copy-start.3
  7.2 0.0 all-gather.4.cloned.1.call-start
  7.2 0.7 all-gather.4.cloned.1.call-update
  7.9 0.0 all-gather.6.cloned.1.call-start
  8.6 1.8 reshape.40
  10.4 1.0 reshape.39
  11.4 0.0 copy-done.3
  11.5 11.3 %all_gather.13 = bf16[4096,64]{0,1:T(8,128)(2,1)S(1)} all-gather(bf16[512,64]{0,1:T(8,128)(2,1)S(1)} %convert_element_type.36), channel_id=1, replica_groups=mesh['dp'=4,'fsdp'=8] {'fsdp'}, dimensions={0}, use_global_device_ids=true | all-gather | bytes 589824 | tf_op jit(solution)/shard_map/all_gather | solution.py:47
  22.8 0.1 fusion.13
  22.9 0.0 copy-done
  22.9 1.4 convolution_convert_fusion.1
  24.3 0.7 fusion.10
  25.0 1.2 fusion.19
  26.3 1.8 divide_convert_fusion
  28.0 0.0 copy-start.1
  28.0 21.2 %all-gather.4.cloned.1.call-done = bf16[4096,512]{1,0:T(8,128)(2,1)} async-done(((bf16[512,512]{1,0:T(8,128)(2,1)}), bf16[4096,512]{1,0:T(8,128)(2,1)}) %all-gather.4.cloned.1.call-update) | async-done | bytes 4194320 | tf_op jit(solution)/shard_map/all_gather | solution.py:42
  49.2 3.4 %fusion.20 = f32[256,512]{1,0:T(8,128)S(1)} fusion(bf16[256,4096]{1,0:T(8,128)(2,1)S(1)} %copy-done, bf16[4096,512]{1,0:T(8,128)(2,1)} %all-gather.4.cloned.1.call-done), kind=kOutput, calls=%fused_computation.36 | convolution fusion | flops 1073741824 | bytes 6815744 | tf_op jit(solution)/shard_map/dot_general | solution.py:40
  52.7 0.0 copy-done.1
  52.7 0.0 copy-done.5
  52.7 0.3 fusion.8
  52.9 0.1 copy.27
  53.1 3.3 %fusion.21 = f32[4,128,4,256]{3,1,2,0:T(8,128)} fusion(bf16[256,4,128,1]{0,2,3,1:T(8,128)(2,1)S(1)} %bitcast.53, bf16[4,4,256,256]{2,3,1,0:T(8,128)(2,1)} %divide_convert_fusion), kind=kOutput, calls=%fused_computation.37 | convolution fusion | flops 268435456 | bytes 4456448 | tf_op jit(solution)/shard_map/kgts,skd->tkgd/dot_general | solution.py:68
  56.4 3.0 copy.19
  59.5 0.0 copy-done.2
  59.5 3.6 %multiply_reduce_fusion = (f32[]{:T(128)}, bf16[256,2048]{1,0:T(8,128)(2,1)}) fusion(f32[256,2048]{1,0:T(8,128)} %copy.19, bf16[256,2048]{1,0:T(8,128)(2,1)S(1)} %copy-done.2, pred[256]{0:T(512)(128)(4,1)S(1)} %iota_compare_fusion.1), kind=kLoop, calls=%fused_computation.7 | loop fusion | flops 3145727 | bytes 4194564 | tf_op jit(solution)/shard_map/reduce_sum | solution.py:73
  63.1 1.5 copy.30
  64.6 2.4 fusion.9
  67.0 0.0 copy-start.6
  67.0 1.8 fusion.1
  68.8 0.0 all-gather.6.cloned.1.call-update
  68.9 0.0 all-reduce.3.cloned.1.call-start
  68.9 0.0 copy-done.6
  68.9 0.9 convolution_multiply_fusion.2
  69.8 0.0 all-reduce.3.cloned.1.call-update
  69.8 0.0 reduce-scatter.2.cloned.1.call-start
  69.9 79.9 %all-gather.6.cloned.1.call-done = f32[16384,64]{0,1:T(8,128)} async-done(((f32[4096,64]{0,1:T(8,128)}), f32[16384,64]{0,1:T(8,128)}) %all-gather.6.cloned.1.call-update) | async-done | bytes 4194320 | tf_op jit(solution)/shard_map/all_gather | solution.py:17
  149.7 6.0 %reshape.43 = f32[4,4096,64]{1,0,2:T(4,128)} reshape(f32[16384,64]{0,1:T(8,128)} %all-gather.6.cloned.1.call-done) | data formatting | bytes 8388608 | tf_op jit(solution)/shard_map/all_gather | solution.py:17
  155.8 5.9 %reduce_sum.28 = f32[4096,64]{0,1:T(8,128)} reduce(f32[4,4096,64]{1,0,2:T(4,128)} %reshape.43, f32[]{:T(128)} %constant.11.clone.1), dimensions={0}, to_apply=%region_2.3 | reduce | flops 786432 | bytes 5242884 | tf_op jit(solution)/shard_map/reduce_sum | solution.py:18
  161.7 0.0 reduce-scatter.2.cloned.1.call-update
  161.7 38.9 %all-reduce = (f32[]{:T(128)}, f32[]{:T(128)}) all-reduce(f32[]{:T(128)S(6)} %convert_element_type.47, f32[]{:T(128)} %get-tuple-element.11), channel_id=1, replica_groups=mesh['dp'=4,'fsdp'=8] {'dp','fsdp'}, use_global_device_ids=true, to_apply=%region_4.5 | all-reduce | flops 2 | bytes 16 | tf_op jit(solution)/shard_map/psum | solution.py:94
  201.9 77.0 %all-reduce.3.cloned.1.call-done = f32[64,512]{1,0:T(8,128)} async-done(((f32[64,512]{1,0:T(8,128)}), f32[64,512]{1,0:T(8,128)}) %all-reduce.3.cloned.1.call-update) | async-done | bytes 131088 | tf_op jit(solution)/shard_map/psum | solution.py:94
  278.9 0.0 copy-done.7
  278.9 2.2 multiply_add_fusion
  281.1 35.8 %reduce-scatter.2.cloned.1.call-done = f32[512,64]{0,1:T(8,128)} async-done(((f32[4096,64]{0,1:T(8,128)}), f32[512,64]{0,1:T(8,128)}) %reduce-scatter.2.cloned.1.call-update) | async-done | bytes 131088 | tf_op jit(solution)/shard_map/reduce_scatter | solution.py:93
  316.9 0.0 copy-done.4
  316.9 0.0 copy-done.8
  316.9 2.2 multiply_add_fusion.1
  (7 shorter events, 0.0 us)
Async XLA Ops:
  7.2 15.8 %copy-start = (bf16[256,4096]{1,0:T(8,128)(2,1)S(1)}, bf16[256,4096]{1,0:T(8,128)(2,1)}, u32[]{:S(2)}) copy-start(bf16[256,4096]{1,0:T(8,128)(2,1)} %param.10) | copy-start | bytes 6291460
  7.2 4.3 %copy-start.3 = (f32[512,64]{0,1:T(8,128)S(1)}, f32[512,64]{0,1:T(8,128)}, u32[]{:S(2)}) copy-start(f32[512,64]{0,1:T(8,128)} %param.16) | copy-start | bytes 393220
  7.2 42.0 %all-gather.4.cloned.1.call-start = ((), (), s32[]{:S(2)}) async-start(), calls=%async_computation.1 | async-start | bytes 4718592 | tf_op jit(solution)/shard_map/all_gather | solution.py:42
  7.9 141.8 %all-gather.6.cloned.1.call-start = ((), (), s32[]{:S(2)}) async-start(), calls=%async_computation.4 | async-start | bytes 5242880 | tf_op jit(solution)/shard_map/all_gather | solution.py:17
  28.0 24.6 %copy-start.1 = (f32[64,512]{1,0:T(8,128)S(1)}, f32[64,512]{1,0:T(8,128)}, u32[]{:S(2)}) copy-start(f32[64,512]{1,0:T(8,128)} %param.17) | copy-start | bytes 393220
  28.0 24.6 %copy-start.5 = (bf16[256,64]{0,1:T(8,128)(2,1)S(1)}, bf16[256,64]{0,1:T(8,128)(2,1)}, u32[]{:S(2)}) copy-start(bf16[256,64]{0,1:T(8,128)(2,1)} %convolution_convert_fusion.1) | copy-start | bytes 98308
  56.4 3.0 copy-start.2
  67.0 1.9 copy-start.6
  68.9 210.0 %all-reduce.3.cloned.1.call-start = ((), (), s32[]{:S(2)}) async-start(), calls=%async_computation.3 | async-start | bytes 262144 | tf_op jit(solution)/shard_map/psum | solution.py:94
  69.8 247.1 %reduce-scatter.2.cloned.1.call-start = ((), (), s32[]{:S(2)}) async-start(), calls=%async_computation.2 | async-start | bytes 1179648 | tf_op jit(solution)/shard_map/reduce_scatter | solution.py:93
  155.8 123.1 %copy-start.7 = (f32[64,512]{1,0:T(8,128)S(1)}, f32[64,512]{1,0:T(8,128)}, u32[]{:S(2)}) copy-start(f32[64,512]{1,0:T(8,128)} %param.19) | copy-start | bytes 393220
  155.8 161.1 %copy-start.4 = (f32[512,64]{0,1:T(8,128)S(1)}, f32[512,64]{0,1:T(8,128)}, u32[]{:S(2)}) copy-start(f32[512,64]{0,1:T(8,128)} %param.16) | copy-start | bytes 393220
  155.8 161.1 %copy-start.8 = (f32[512,64]{0,1:T(8,128)S(1)}, f32[512,64]{0,1:T(8,128)}, u32[]{:S(2)}) copy-start(f32[512,64]{0,1:T(8,128)} %param.18) | copy-start | bytes 393220
Sparse Core Ops, SparseCore 0:
  9.9 39.2 all-gather.3
  69.0 80.7 all-gather.5
  155.9 122.9 all-reduce.2
  281.9 34.9 reduce-scatter.1
